TPU v7x, 256 devices: a 2x2x32 block of a 4x8x32 slice. The times are simulated.
256 devices in a mesh: groups: 4 (over x, y), seq: 32 (over z), pd: 2 (over core).
Axes of the slice: x: 2, y: 2, z: 32, core: 2. Of those that a mesh axis runs over, the one named last changes fastest.
The devices are a block of a 4x8x32 slice.
Arguments:
- streams: bfloat16 [32768, 4, 7168], P(('groups', 'seq'), None, 'pd'), parts along dimension 0, may hold values from -6 to 6
- mix_first: bfloat16 [4, 7168, 24], P(None, 'pd'), may hold values from -0.03125 to 0.03125
- first_layer_bias: float32 [24], replicated, may hold values from -3 to 3
- pre_second: bfloat16 [4, 7168, 4], P(None, 'pd'), may hold values from -0.03125 to 0.03125
- bias_second: float32 [4], replicated, may hold values from -3 to 3
- w_latent: bfloat16 [2, 7168, 576], P(None, ('pd', 'seq')), may hold values from -0.0625 to 0.0625
- latent_gain: float32 [2, 512], replicated, may hold values from 0.5 to 1.5
- out_weight: bfloat16 [512, 7168], P(None, 'pd'), may hold values from -0.25 to 0.25
- span_slot: int32 [256], P('groups'), parts along dimension 0, may hold values from 0 to 63, each once
- block_owner: int32 [128], P('groups'), parts along dimension 0, may hold values from 0 to 31, each once
- prompt_length: int32 [4], P('groups'), parts along dimension 0, may hold values from 4096 to 8192
Outputs:
- cache: bfloat16 [2, 32768, 576], P(None, ('groups', 'seq')), parts along dimension 1
There are 4 independent parts, one for each index of `groups`. A program takes and returns all parts, laid end to end along the dimension named above; an argument that names none is the same for every part. Nothing has to cross between parts.
Inputs may be any that keep to these rules, and one draw needn't show every extreme that they name: span_slot is a permutation; slot q lies in rows q * 128 to q * 128 + 127 of streams. block_owner is a permutation.
All inputs are finite; a program needn't handle non-finite values.
Results may differ from a plain program's by a relative error of at most 0.0058.
Values may be sent and summed in bfloat16 or wider, within the bound.
A program may use at most 128 MiB of HBM per device.

v0:
```python
import jax
import jax.numpy as jnp
from jax import lax
from jax.sharding import PartitionSpec as P

LAT = 512
ROPE = 64
RESIDUAL_WAYS = 4
SINK = 20


EPSILON = 1e-06
THETA = 10000.0


def sent_to_all(x, axis):
    copies = jnp.broadcast_to(x, (lax.axis_size(axis), *x.shape))
    return lax.all_to_all(copies, axis, split_axis=0, concat_axis=0, tiled=True)


def taken_together(x, axis):
    return sent_to_all(x, axis).sum(axis=0)


def packed_total(arrays, axis):
    ends = [0]
    for a in arrays:
        ends.append(ends[-1] + a.size)
    so_far = taken_together(jnp.concatenate([a.ravel() for a in arrays]), axis)
    return tuple((so_far[b:e].reshape(a.shape) for a, b, e in zip(arrays, ends, ends[1:])))


def doubly_stochastic_normalize(blend_scores_raw):

    def one_sweep(turn_index, matrix):
        matrix = matrix / jnp.sum(matrix, axis=2, keepdims=True)
        return matrix / jnp.sum(matrix, axis=1, keepdims=True)

    return lax.fori_loop(0, SINK, one_sweep, jnp.exp(blend_scores_raw))


def combine(weights, stream_block):
    weighted = weights[:, 0, None] * stream_block[:, 0, :].astype(jnp.float32)
    for stream_index in range(1, RESIDUAL_WAYS):
        weighted = weighted + weights[:, stream_index, None] * stream_block[
            :, stream_index, :
        ].astype(jnp.float32)
    return weighted


def coefficients(stream_block, weights, offsets):
    flattened = stream_block.reshape(stream_block.shape[0], -1)
    partial_value = jnp.dot(
        flattened, weights.reshape(flattened.shape[1], -1), preferred_element_type=jnp.float32
    )
    elementwise_power_two = jnp.sum(jnp.square(flattened.astype(jnp.float32)), axis=1)
    projected, square_sum = packed_total((partial_value, elementwise_power_two), "pd")
    entry_count = flattened.shape[1] * lax.axis_size("pd")
    rms_scale = jnp.sqrt(square_sum / entry_count + EPSILON)
    return projected / rms_scale[:, None] + offsets[None, :]


def cache_entry(summed, places, gain_row):
    latent = summed[:, :LAT]
    mean_square = jnp.mean(latent * latent, axis=1, keepdims=True)
    normed = latent * lax.rsqrt(mean_square + EPSILON) * gain_row[None, :]
    half_rope = ROPE // 2
    frequency = THETA ** (-jnp.arange(half_rope, dtype=jnp.float32) / half_rope)
    angles = places.astype(jnp.float32)[:, None] * frequency[None, :]
    first_half = summed[:, LAT : LAT + half_rope]
    second = summed[:, LAT + half_rope :]
    cosine_table = jnp.cos(angles)
    sine_values = jnp.sin(angles)
    rotated = jnp.concatenate(
        [
            first_half * cosine_table - second * sine_values,
            second * cosine_table + first_half * sine_values,
        ],
        axis=1,
    )
    return jnp.concatenate([normed, rotated], axis=1).astype(jnp.bfloat16)


def on_device(
    streams,
    mix_first,
    first_layer_bias,
    pre_second,
    bias_second,
    w_latent,
    latent_gain,
    out_weight,
    span_slot,
    block_owner,
    prompt_length,
):
    tokens_here = streams.shape[0]
    span_rows = tokens_here // 2
    seq_count = lax.axis_size("seq")
    my_index = lax.axis_index("seq")
    own_slots = 2 * my_index + jnp.arange(2, dtype=jnp.int32)
    span_ids = jnp.arange(2 * seq_count, dtype=jnp.int32)
    own_spans = jnp.sum(
        span_ids[None, :] * (span_slot[None, :] == own_slots[:, None]).astype(jnp.int32), axis=1
    )
    places = (
        own_spans[:, None] * span_rows + jnp.arange(span_rows, dtype=jnp.int32)[None, :]
    ).reshape(-1)
    in_prompt = places < prompt_length[0]
    my_block = jnp.sum(
        jnp.arange(seq_count, dtype=jnp.int32) * (block_owner == my_index).astype(jnp.int32)
    )
    wanted_slots = span_slot[2 * my_block + jnp.arange(2, dtype=jnp.int32)]

    def latent_of(hidden, layer_index):
        partial_value = jnp.dot(
            hidden,
            lax.all_gather(w_latent[layer_index], "seq", axis=0, tiled=True),
            preferred_element_type=jnp.float32,
        )
        summed = taken_together(partial_value, "pd")
        return cache_entry(summed, places, latent_gain[layer_index])

    def masked(entry_rows):
        return jnp.where(in_prompt[:, None], entry_rows, jnp.zeros((), jnp.bfloat16))

    blend_weight = coefficients(streams, mix_first, first_layer_bias)
    pre_gate = jax.nn.sigmoid(blend_weight[:, :RESIDUAL_WAYS])
    post_gate = 2.0 * jax.nn.sigmoid(blend_weight[:, RESIDUAL_WAYS : 2 * RESIDUAL_WAYS])
    residual_blend_matrix = doubly_stochastic_normalize(
        blend_weight[:, 2 * RESIDUAL_WAYS :].reshape(-1, RESIDUAL_WAYS, RESIDUAL_WAYS)
    )
    hidden = combine(pre_gate, streams).astype(jnp.bfloat16)
    entry_first = latent_of(hidden, 0)
    branch = jnp.dot(entry_first[:, :LAT], out_weight, preferred_element_type=jnp.float32)
    updated = jnp.stack(
        [
            combine(residual_blend_matrix[:, stream_index, :], streams)
            + post_gate[:, stream_index, None] * branch
            for stream_index in range(RESIDUAL_WAYS)
        ],
        axis=1,
    ).astype(jnp.bfloat16)
    second_coef = coefficients(updated, pre_second, bias_second)
    hidden_second = combine(jax.nn.sigmoid(second_coef), updated).astype(jnp.bfloat16)
    entry_second = latent_of(hidden_second, 1)
    stacked = jnp.stack([masked(entry_first), masked(entry_second)])
    collected = jnp.zeros_like(stacked)
    shard_piece = lax.all_gather(stacked, "seq", axis=1, tiled=True)
    piece_rows = shard_piece.shape[1]
    span_parts = []
    for lane in range(2):
        offset = wanted_slots[lane] * span_rows
        inside = jnp.logical_and(offset >= 0, offset + span_rows <= piece_rows)
        clipped = jnp.clip(offset, 0, piece_rows - span_rows)
        sliced = lax.dynamic_slice_in_dim(shard_piece, clipped, span_rows, 1)
        span_parts.append(
            jnp.where(inside, sliced, collected[:, lane * span_rows : (lane + 1) * span_rows])
        )
    return jnp.concatenate(span_parts, axis=1)


def solution(mesh):
    placed = (
        P(("groups", "seq"), None, "pd"),
        P(None, "pd", None),
        P(),
        P(None, "pd", None),
        P(),
        P(None, ("pd", "seq"), None),
        P(),
        P(None, "pd"),
        P("groups"),
        P("groups"),
        P("groups"),
    )
    return jax.shard_map(
        on_device,
        mesh=mesh,
        in_specs=placed,
        out_specs=P(None, ("groups", "seq"), None),
        check_vma=False,
    )
```

profile of v0, /device:TPU:38, one launch (start us, length us, event | category | flops | bytes accessed | tf_op | source)
XLA Modules:
  0.0 583.2 jit_solution(3354800891817134645)
XLA Ops:
  6.5 0.0 copy-start
  6.6 1.8 fusion.78
  8.3 0.1 all-gather.8.cloned.1.call-update
  8.4 0.0 copy-done
  8.4 5.2 convolution_bitcast_fusion
  13.6 0.1 reshape.292
  13.7 0.0 copy-start.7
  13.7 8.0 %multiply_reduce_fusion.1 = f32[256]{0:T(256)S(1)} fusion(bf16[256,4,3584]{2,1,0:T(4,128)(2,1)} %param.13), kind=kLoop, calls=%fused_computation.4 | loop fusion | flops 11009792 | bytes 7341056 | tf_op jit(solution)/shard_map/reduce_sum | solution.py:56
  21.7 0.6 broadcast_in_dim.23
  22.4 3.3 all-to-all-start
  25.7 0.1 all-gather.10.cloned.1.call-start
  25.8 0.7 all-gather.10.cloned.1.call-update
  26.5 0.1 all-gather.6.cloned.1.call-start
  26.6 0.5 all-to-all-done
  27.1 0.1 reduce_sum.111
  27.2 0.1 reshape.293
  27.3 0.1 copy.68
  27.4 0.1 divide_add_fusion
  27.5 1.7 while.10
  29.2 0.0 copy-start.2
  29.2 0.0 copy-start.6
  29.3 7.4 %copy.65 = bf16[256,4,3584]{2,0,1:T(8,128)(2,1)} copy(bf16[256,4,3584]{2,1,0:T(4,128)(2,1)} %param.13) | data formatting | bytes 14680064 | tf_op args[0]
  37.3 0.2 fusion.67
  37.5 0.1 compare_bitcast_fusion
  37.6 0.1 convert_bitcast_fusion
  37.7 121.9 %all-gather.8.cloned.1.call-done = bf16[1,3584,576]{2,1,0:T(8,128)(2,1)} async-done(((bf16[1,112,576]{2,1,0:T(8,128)(2,1)}), bf16[1,3584,576]{2,1,0:T(8,128)(2,1)}) %all-gather.8.cloned.1.call-update) | async-done | bytes 4128784 | tf_op jit(solution)/shard_map/all_gather | solution.py:118
  159.6 8.4 %fusion.2 = f32[256,576]{0,1:T(8,128)S(1)} fusion(bf16[1,3584,576]{2,1,0:T(8,128)(2,1)} %all-gather.8.cloned.1.call-done, f32[256]{0:T(256)S(1)} %bitcast.168, f32[256]{0:T(256)S(1)} %bitcast.167, f32[256]{0:T(256)S(1)} %bitcast.166, f32[256]{0:T(256)S(1)} %bitcast.169, bf16[256,4,3584]{2,0,1:T(8,128)(2,1)} %copy.65), kind=kOutput, calls=%fused_computation.28 | convolution fusion | flops 1067974656 | bytes 12062720 | tf_op jit(solution)/shard_map/dot_general | solution.py:116
  168.0 0.1 broadcast_in_dim.24
  168.1 4.7 all_to_all.22
  172.8 0.1 reduce_sum.112
  173.0 0.1 multiply_reduce_fusion.3
  173.1 0.0 slice-start.1
  173.1 7.9 %fusion.12 = (bf16[256,3584]{1,0:T(8,128)(2,1)S(1)}, bf16[256,3584]{1,0:T(8,128)(2,1)S(1)}, f32[256,3584]{1,0:T(8,128)S(1)}) fusion(f32[256]{0:T(256)S(1)} %bitcast.160, f32[256]{0:T(256)S(1)} %bitcast.163, f32[256]{0:T(256)S(1)} %bitcast.164, f32[256]{0:T(256)S(1)} %bitcast.165, f32[256]{0:T(256)S(1)} %bitcast.162, bf16[256,4,3584]{2,0,1:T(8,128)(2,1)} %copy.65, ...), kind=kOutput, calls=%fused_computation.38 | convolution fusion | flops 961937408 | bytes 18887680 | tf_op jit(solution)/shard_map/dot_general | solution.py:135
  181.0 0.0 copy-start.9
  181.0 4.1 fusion.17
  185.2 1.2 copy-done.3
  186.4 2.0 fusion.38
  188.5 0.1 reshape.294
  188.6 0.0 copy-start.8
  188.6 4.0 multiply_reduce_fusion
  192.7 3.7 all_to_all.23
  196.4 0.1 reshape.295
  196.6 0.1 copy.75
  196.6 0.0 copy-done.8
  196.7 0.1 add_divide_fusion
  196.8 0.1 fusion.76
  196.9 95.3 %all-gather.10.cloned.1.call-done = bf16[1,3584,576]{2,1,0:T(8,128)(2,1)} async-done(((bf16[1,112,576]{2,1,0:T(8,128)(2,1)}), bf16[1,3584,576]{2,1,0:T(8,128)(2,1)}) %all-gather.10.cloned.1.call-update) | async-done | bytes 4128784 | tf_op jit(solution)/shard_map/all_gather | solution.py:118
  292.2 6.6 %fusion = f32[256,576]{0,1:T(8,128)S(1)} fusion(bf16[1,3584,576]{2,1,0:T(8,128)(2,1)} %all-gather.10.cloned.1.call-done, bf16[256,3584]{1,0:T(8,128)(2,1)} %copy-done.5, bf16[256,3584]{1,0:T(8,128)(2,1)} %copy-done.3, bf16[256,3584]{1,0:T(8,128)(2,1)S(1)} %get-tuple-element.28, bf16[256,3584]{1,0:T(8,128)(2,1)} %copy-done.4, f32[256]{0:T(256)S(1)} %bitcast.175, ...), kind=kOutput, calls=%fused_computation.26 | convolution fusion | flops 1067974656 | bytes 12062720 | tf_op jit(solution)/shard_map/dot_general | solution.py:116
  298.8 0.1 broadcast_in_dim.27
  298.9 4.7 all_to_all.24
  303.6 0.1 reduce_sum.116
  303.7 0.1 multiply_reduce_fusion.2
  303.8 0.1 fusion.39
  304.0 0.2 fusion.59
  304.2 0.1 maximum_select_fusion
  304.3 0.9 pad_maximum_fusion.4
  305.2 0.1 all-gather.6.cloned.1.call-update
  305.2 0.7 fusion.72
  306.7 0.6 gather_fusion
  307.3 0.6 fusion.87
  309.2 265.1 %all-gather.6.cloned.1.call-done = bf16[2,8192,576]{1,2,0:T(8,128)(2,1)} async-done(((bf16[2,256,576]{1,2,0:T(8,128)(2,1)}), bf16[2,8192,576]{1,2,0:T(8,128)(2,1)}) %all-gather.6.cloned.1.call-update) | async-done | bytes 18874384 | tf_op jit(solution)/shard_map/all_gather | solution.py:149
  574.3 1.5 dynamic-slice_select_fusion.1
  575.8 0.9 pad_maximum_fusion.5
  576.7 0.0 copy-done.1
  (101 shorter events, 1.5 us)
Async XLA Ops:
  6.5 1.9 copy-start
  6.6 153.1 %all-gather.8.cloned.1.call-start = ((), (), s32[]{:S(2)}) async-start(), calls=%async_computation.5 | async-start | bytes 4730880 | tf_op jit(solution)/shard_map/all_gather | solution.py:118
  13.7 13.6 %copy-start.7 = (f32[24]{0:T(128)S(1)}, f32[24]{0:T(128)}, u32[]{:S(2)}) copy-start(f32[24]{0:T(128)} %param.15) | copy-start | bytes 292
  22.4 4.7 all-to-all-start
  25.7 266.6 %all-gather.10.cloned.1.call-start = ((), (), s32[]{:S(2)}) async-start(), calls=%async_computation.6 | async-start | bytes 4730880 | tf_op jit(solution)/shard_map/all_gather | solution.py:118
  26.5 547.8 %all-gather.6.cloned.1.call-start = ((), (), s32[]{:S(2)}) async-start(), calls=%async_computation.4 | async-start | bytes 19464192 | tf_op jit(solution)/shard_map/all_gather | solution.py:149
  29.2 8.0 %copy-start.2 = (s32[64]{0:T(128)S(1)}, s32[64]{0:T(128)}, u32[]{:S(2)}) copy-start(s32[64]{0:T(128)} %param.21) | copy-start | bytes 772
  29.2 8.4 %copy-start.6 = (f32[2,512]{1,0:T(2,128)S(1)}, f32[2,512]{1,0:T(2,128)}, u32[]{:S(2)}) copy-start(f32[2,512]{1,0:T(2,128)} %param.19) | copy-start | bytes 12292
  173.1 7.9 %slice-start = ((s8[7340032]{0:T(1024)(128)(4,1)}), s8[4194304]{0:T(1024)(128)(4,1)S(1)}, s32[]{:S(2)}) async-start(s8[7340032]{0:T(1024)(128)(4,1)} %bitcast.137), calls=%async_computation.7 | async-start | bytes 8388608
  173.1 7.9 %slice-start.1 = ((s8[7340032]{0:T(1024)(128)(4,1)}), s8[3145728]{0:T(1024)(128)(4,1)S(1)}, s32[]{:S(2)}) async-start(s8[7340032]{0:T(1024)(128)(4,1)} %bitcast.137), calls=%async_computation.8 | async-start | bytes 6291456
  181.0 4.2 copy-start.4
  181.0 4.2 copy-start.5
  181.0 5.4 copy-start.9
  185.2 1.2 copy-start.3
  188.6 8.1 %copy-start.8 = (f32[4]{0:T(128)S(1)}, f32[4]{0:T(128)}, u32[]{:S(2)}) copy-start(f32[4]{0:T(128)} %param.17) | copy-start | bytes 52
  303.6 1.6 copy-start.10
  303.6 273.1 %copy-start.1 = (bf16[4,3584,24]{1,2,0:T(8,128)(2,1)S(1)}, bf16[4,3584,24]{1,2,0:T(8,128)(2,1)}, u32[]{:S(2)}) copy-start(bf16[4,3584,24]{1,2,0:T(8,128)(2,1)} %param.14) | copy-start | bytes 2064388
Sparse Core Ops, SparseCore 0:
  9.1 150.4 all-gather.7
  161.4 130.7 all-gather.9
  305.4 268.8 all-gather.5
where the time goes:
time: 584 us; the launch traced here: 583 us
  waiting for transfers between devices  484 us (83%)
  matrix products  30.1 us (5%)
  other arithmetic  23.1 us (4%)
  between operations  16.2 us (3%)
  local copies, waits for them, and re-layouts  13.2 us (2%)
  blocking collectives  13.1 us (2%)
    all_gather x1, waiting for transfers between devices, on_device(): shard_piece = lax.all_gather(stacked, 'seq', axis=1, tiled=True)  265 us
    all_gather x2, waiting for transfers between devices, latent_of(): lax.all_gather(w_latent[layer_index], 'seq', axis=0, tiled=True)  217 us
    dot_general x2, matrix products, latent_of(): jnp.dot(hidden, lax.all_gather(w_latent[layer_index], 'seq', axis=0, tile...  15 us
    all_to_all x3, blocking collectives, sent_to_all(): return lax.all_to_all(copies, axis, split_axis=0, concat_axis=0, tiled=True)  13.1 us
    reduce_sum x2, other arithmetic, coefficients(): jnp.sum(jnp.square(flattened.astype(jnp.float32)), axis=1)  12 us
  transfers between devices with their start and end apart: 4, of which 4 were waited for; matrix products, arithmetic and copies ran while one was open for 9% of the time, Pallas kernels for 0%

commit v1 on v0

v1 whole, which is shorter than its diff:
```python
import functools
import math

import jax
import jax.numpy as jnp
import numpy as np
from jax import lax
from jax.experimental import pallas as pl
from jax.experimental.pallas import tpu as pltpu
from jax.sharding import PartitionSpec as P

LAT = 512
ROPE = 64
WAYS = 4
SINK = 20
EPSILON = 1e-06
THETA = 10000.0

LANES = 128
MESH = pl.DeviceIdType.MESH
BF16 = jnp.bfloat16
F32 = jnp.float32

FIRST = (0, 1, 2)
SECOND = (3, 4)
CROSS = {0: ("x", 5), 1: ("y", 6), 3: ("x", 7), 4: ("y", 8)}
ORDER = ((0, 1, 5, 6), (3, 4, 7, 8))


def kernel(
    n,
    ny,
    streams,
    mix,
    pre,
    w_in,
    out_w,
    bias1,
    bias2,
    gain,
    freq,
    slots,
    owners,
    length,
    out,
    raw,
    s4,
    wg,
    wl,
    mp,
    pp,
    hid,
    ow,
    cacc,
    cgot,
    ctr,
    cb,
    down,
    got,
    ent1,
    branch,
    trig,
    es,
    er,
    r1_first,
    r1_second,
    s2,
    r2,
    rp,
    rr1,
    rs2,
    rr2,
    rrp,
    ov,
    table,
    load_sem,
    zsend,
    zrecv,
    xsend,
    xrecv,
    psend,
    precv,
    asend,
    arecv,
    osem,
):
    me = lax.axis_index("seq")
    group = lax.axis_index("groups")
    core = lax.axis_index("pd")
    right = lax.rem(me + 1, n)
    left = lax.rem(me + n - 1, n)
    par_y = lax.rem(group, 2)
    par_x = lax.rem(lax.div(group, ny), 2)
    y_mate = group + 1 - 2 * par_y
    x_mate = group + (1 - 2 * par_x) * ny
    tokens, width = s4.shape[1:]
    r1 = (r1_first, r1_second)
    chunk = w_in.shape[1]
    span = tokens // 2
    cols = width // LANES
    entries = WAYS * width * 2

    barrier = pltpu.get_barrier_semaphore()
    for place in ({"seq": right}, {"seq": left}, {"groups": y_mate}, {"groups": x_mate}, {"pd": 1 - core}):
        pl.semaphore_signal(barrier, inc=1, device_id=place, device_id_type=MESH)

    def w_load():
        return pltpu.make_async_copy(w_in, wl, load_sem.at[0])

    def s_load(block):
        return pltpu.make_async_copy(
            streams.at[:, :, pl.ds(block * LANES, LANES)], raw.at[block], load_sem.at[1 + block]
        )

    def m_load(j):
        return pltpu.make_async_copy(mix.at[j], mp.at[pl.ds(j * 32, 24)], load_sem.at[1 + cols + j])

    def o_load():
        return pltpu.make_async_copy(out_w, ow, load_sem.at[5 + cols])

    w_load().start()
    for j in range(WAYS):
        m_load(j).start()
    for block in range(cols):
        s_load(block).start()
    o_load().start()

    own = pl.ds(pl.multiple_of(me * chunk, 16), chunk)
    w_load().wait()
    for layer in range(2):
        blocks = [wl[layer, :, b * LANES : (b + 1) * LANES] for b in range(4)]
        a_mine = jnp.where(par_x == 0, blocks[0], blocks[1])
        a_other = jnp.where(par_x == 0, blocks[1], blocks[0])
        b_mine = jnp.where(par_y == 0, blocks[2], blocks[3])
        b_other = jnp.where(par_y == 0, blocks[3], blocks[2])
        for slot, value in zip(ORDER[layer], (a_mine, b_mine, a_other, b_other)):
            wg[slot, own, :] = value
    wg[2, own, :] = jnp.concatenate([wl[0, :, LAT:], wl[1, :, LAT:]], axis=1)
    pl.semaphore_wait(barrier, 5)

    half = n // 2
    steps = (half, n - 1 - half)

    def z_copy(way, step, slot, source):
        rows = pl.ds(pl.multiple_of(source * chunk, 16), chunk)
        return pltpu.make_async_remote_copy(
            wg.at[slot, rows],
            wg.at[slot, rows],
            zsend.at[way, slot],
            zrecv.at[way, step - 1, slot],
            device_id={"seq": right if way == 0 else left},
            device_id_type=MESH,
        )

    def cross_copy(slot, source):
        axis, other = CROSS[slot]
        rows = pl.ds(pl.multiple_of(source * chunk, 16), chunk)
        return pltpu.make_async_remote_copy(
            wg.at[slot, rows],
            wg.at[other, rows],
            xsend.at[other - 5],
            xrecv.at[other - 5],
            device_id={"groups": x_mate if axis == "x" else y_mate},
            device_id_type=MESH,
        )

    def z_start(which):
        for slot in which:
            for way in (0, 1):
                z_copy(way, 1, slot, me).start()

    def z_step(which, step):
        for slot in which:
            for way in (0, 1):
                if step > steps[way]:
                    continue
                source = lax.rem(me + (n - step if way == 0 else step), n)
                z_copy(way, step, slot, source).wait_recv()
                if step < steps[way]:
                    z_copy(way, step + 1, slot, source).start()
                if slot in CROSS:
                    cross_copy(slot, source).start()

    def cross_whole(other):
        rows = wg.at[other, pl.ds(0, (n - 1) * chunk)]
        return pltpu.make_async_remote_copy(
            rows, rows, xsend.at[other - 5], xrecv.at[other - 5], device_id={"groups": x_mate}, device_id_type=MESH
        )

    def z_whole(way, slot):
        rows = wg.at[slot, pl.ds(0, steps[way] * chunk)]
        return pltpu.make_async_remote_copy(
            rows, rows, zsend.at[way, slot], zrecv.at[way, 0, slot], device_id={"seq": right}, device_id_type=MESH
        )

    def service(step):
        if step <= half:
            z_step(FIRST, step)
            z_step(SECOND, step)

    z_start(FIRST)
    z_start(SECOND)

    for j in range(WAYS):
        mp[j * 32 + 24 : j * 32 + 32, :] = jnp.zeros((8, width), BF16)
    row_id = lax.broadcasted_iota(jnp.int32, (256, 256), 0)
    col_id = lax.broadcasted_iota(jnp.int32, (256, 256), 1)
    sort = jnp.where(col_id == (row_id & 63) * 4 + (row_id >> 6), 1.0, 0.0).astype(BF16)
    lane_way = (
        lax.broadcasted_iota(jnp.int32, (256, LANES), 1) >> 5
        == lax.broadcasted_iota(jnp.int32, (256, LANES), 0) >> 6
    )
    cacc[...] = jnp.zeros_like(cacc)
    for j in range(WAYS):
        m_load(j).wait()

    def planes(q):
        for block in (2 * q, 2 * q + 1):
            s_load(block).wait()

        def body(part, carry):
            rows = pl.ds(pl.multiple_of(part * 64, 64), 64)
            pieces = [raw[block, pl.ds(part * 64, 64)].reshape(256, LANES) for block in (2 * q, 2 * q + 1)]
            sorted_rows = jnp.dot(sort, jnp.concatenate(pieces, axis=1), preferred_element_type=F32)
            narrow = sorted_rows.astype(BF16)
            for j in range(WAYS):
                s4[j, rows, q * 256 : q * 256 + 256] = narrow[j * 64 : j * 64 + 64]
            picked = lax.dot_general(
                narrow, mp[:, q * 256 : q * 256 + 256], (((1,), (1,)), ((), ())), preferred_element_type=F32
            )
            picked = jnp.where(lane_way, picked, 0.0)
            square = sorted_rows * sorted_rows
            square = square[:, :LANES] + square[:, LANES:]
            cacc[0, rows, :] += picked[:64] + picked[64:128] + picked[128:192] + picked[192:]
            cacc[1, rows, :] += square[:64] + square[64:128] + square[128:192] + square[192:]
            return carry

        lax.fori_loop(0, tokens // 64, body, 0)

    def pair_copy(source, target, index):
        return pltpu.make_async_remote_copy(
            source, target, psend.at[index], precv.at[index], device_id={"pd": 1 - core}, device_id_type=MESH
        )

    def own_span(which):
        slot = 2 * me + which
        return lax.fori_loop(
            0, 2 * n, lambda c, found: jnp.where(slots[c] == slot, c, found), jnp.int32(0)
        )

    spans_here = [own_span(0), own_span(1)]

    def trig_tables():
        for which in range(2):
            base = spans_here[which] * span
            place = (lax.broadcasted_iota(jnp.int32, (span, LANES), 0) + base).astype(F32)
            angle = place * freq[...]
            sign = jnp.where((lax.broadcasted_iota(jnp.int32, (span, LANES), 1) >> 5) & 1 == 0, -1.0, 1.0)
            trig[0, which * span : (which + 1) * span, :] = jnp.cos(angle)
            trig[1, which * span : (which + 1) * span, :] = jnp.sin(angle) * sign

    def wanted_table():
        def body(i, carry):
            block = jnp.int32(0)
            for b in range(n):
                block = jnp.where(owners[b] == i, b, block)
            table[2 * i] = slots[2 * block]
            table[2 * i + 1] = slots[2 * block + 1]
            return carry

        lax.fori_loop(0, n, body, 0)

    def first_gates():
        total = cacc[0] + cgot[0]
        total = total + pltpu.roll(total, 64, 1)
        total = total + pltpu.roll(total, 32, 1)
        square = jnp.sum(cacc[1] + cgot[1], axis=1, keepdims=True)
        scale = 1.0 / jnp.sqrt(square / entries + EPSILON)
        ctr[...] = jnp.transpose(total * scale + bias1[...])
        gates = jax.nn.sigmoid(ctr[0:8, :])
        doubled = lax.broadcasted_iota(jnp.int32, gates.shape, 0) >= WAYS
        gates = jnp.where(doubled, 2.0 * gates, gates)
        start = jnp.exp(ctr[8:24, :])
        matrix = tuple(start[k : k + 1, :] for k in range(WAYS * WAYS))

        def sweep(turn, m):
            m = list(m)
            for i in range(WAYS):
                inv = 1.0 / (m[4 * i] + m[4 * i + 1] + m[4 * i + 2] + m[4 * i + 3])
                for j in range(WAYS):
                    m[4 * i + j] = m[4 * i + j] * inv
            for j in range(WAYS):
                inv = 1.0 / (m[j] + m[4 + j] + m[8 + j] + m[12 + j])
                for i in range(WAYS):
                    m[4 * i + j] = m[4 * i + j] * inv
            return tuple(m)

        matrix = lax.fori_loop(0, SINK, sweep, matrix)
        ctr[0:8, :] = gates
        for k in range(WAYS * WAYS):
            ctr[8 + k : 9 + k, :] = matrix[k]

    def spread_gates():
        back = jnp.transpose(ctr[...])
        for k in range(24):
            cb[k] = jnp.broadcast_to(back[:, k : k + 1], (tokens, LANES))

    def combine_rows(lo, hi, first):
        def body(part, carry):
            rows = pl.ds(pl.multiple_of(part * 16, 16), 16)
            for tile in range(width // 512):
                c0 = tile * 512
                total = None
                for j in range(WAYS):
                    w = cb[first + j, rows, :]
                    term = jnp.concatenate([w] * 4, axis=1) * s4[j, rows, c0 : c0 + 512].astype(F32)
                    total = term if total is None else total + term
                hid[rows, c0 : c0 + 512] = total.astype(BF16)
            return carry

        lax.fori_loop(lo, hi, body, 0)

    def down_project(layer):
        slot_list = ORDER[layer] + (2,)

        def body(k, carry):
            k0 = pl.multiple_of(k * 512, 512)
            left_side = hid[:, pl.ds(k0, 512)]
            for c0, group_of in ((0, slot_list[0:2]), (256, slot_list[2:4]), (512, slot_list[4:5])):
                right_side = [wg[slot, pl.ds(k0, 512), :] for slot in group_of]
                right_side = right_side[0] if len(right_side) == 1 else jnp.concatenate(right_side, axis=1)
                part = jnp.dot(left_side, right_side, preferred_element_type=F32)
                wide = LANES * len(group_of)
                down[layer, :, c0 : c0 + wide] += part
            return carry

        down[layer] = jnp.zeros_like(down[layer])
        lax.fori_loop(0, width // 512, body, 0)

    def entry(layer):
        def body(part, carry):
            rows = pl.ds(pl.multiple_of(part * 32, 32), 32)
            summed = down[layer, rows, :] + got[layer, rows, :]
            latent = summed[:, :LAT]
            mean_square = jnp.sum(latent * latent, axis=1, keepdims=True) / LAT
            scale = lax.rsqrt(mean_square + EPSILON)
            m = [summed[:, b * LANES : (b + 1) * LANES] * scale for b in range(4)]
            blocks = [
                jnp.where(par_x == 0, m[0], m[2]),
                jnp.where(par_x == 0, m[2], m[0]),
                jnp.where(par_y == 0, m[1], m[3]),
                jnp.where(par_y == 0, m[3], m[1]),
            ]
            blocks = [blocks[b] * gain[layer : layer + 1, b * LANES : (b + 1) * LANES] for b in range(4)]
            which = lax.div(part, 4)
            base = jnp.where(which == 0, spans_here[0], spans_here[1]) * span + lax.rem(part, 4) * 32
            place = lax.broadcasted_iota(jnp.int32, (32, LANES), 0) + base
            inside = place < length[0]
            tile0 = pl.multiple_of(lax.rem(part, 4) * 4, 4)
            for h in range(2):
                block = jnp.where(core == 0, blocks[2 * h], blocks[2 * h + 1])
                es[layer, h, which, pl.ds(tile0, 4)] = (
                    jnp.where(inside, block, 0.0).reshape(4, 8, LANES).astype(BF16)
                )
            if layer == 0:
                ent1[rows, :] = jnp.concatenate(blocks, axis=1).astype(BF16)
            else:
                lane = lax.broadcasted_iota(jnp.int32, (32, LANES), 1)
                key = jnp.where(
                    lane < ROPE, down[0, rows, LAT:] + got[0, rows, LAT:], summed[:, LAT:]
                )
                swapped = jnp.where((lane >> 5) & 1 == 0, pltpu.roll(key, 96, 1), pltpu.roll(key, 32, 1))
                turned = key * trig[0, rows, :] + swapped * trig[1, rows, :]
                er[which, pl.ds(tile0, 4)] = jnp.where(inside, turned, 0.0).reshape(4, 8, LANES).astype(BF16)
            return carry

        lax.fori_loop(0, tokens // 32, body, 0)

    def update_tile(tile):
        c0 = tile * 512
        branch[...] = jnp.dot(ent1[...], ow[:, c0 : c0 + 512], preferred_element_type=F32)

        def body(part, carry):
            rows = pl.ds(pl.multiple_of(part * 16, 16), 16)
            for sub in range(4):
                d0 = c0 + sub * LANES
                old = [s4[j, rows, d0 : d0 + LANES].astype(F32) for j in range(WAYS)]
                add = branch[rows, sub * LANES : (sub + 1) * LANES]
                square = None
                for i in range(WAYS):
                    total = cb[WAYS + i, rows, :] * add
                    for j in range(WAYS):
                        total = total + cb[8 + 4 * i + j, rows, :] * old[j]
                    narrow = total.astype(BF16)
                    s4[i, rows, d0 : d0 + LANES] = narrow
                    wide = narrow.astype(F32)
                    square = wide * wide if square is None else square + wide * wide
                cacc[1, rows, :] += square
            return carry

        lax.fori_loop(0, tokens // 16, body, 0)
        total = None
        for j in range(WAYS):
            part = lax.dot_general(
                s4[j, :, c0 : c0 + 512],
                pp[j * 8 : j * 8 + 8, c0 : c0 + 512].astype(BF16),
                (((1,), (1,)), ((), ())),
                preferred_element_type=F32,
            )
            total = part if total is None else total + part
        cacc[0, :, 0:8] += total

    def second_gates():
        total = cacc[0] + cgot[2]
        square = jnp.sum(cacc[1] + cgot[3], axis=1, keepdims=True)
        scale = 1.0 / jnp.sqrt(square / entries + EPSILON)
        for k in range(WAYS):
            gate = jax.nn.sigmoid(total[:, k : k + 1] * scale + bias2[k])
            cb[k] = jnp.broadcast_to(gate, (tokens, LANES))

    def all_send(source_of, target, index):
        def body(d, carry):
            j = lax.rem(me + d, n)
            pltpu.make_async_remote_copy(
                source_of(j), target, asend.at[index], arecv.at[index], device_id={"seq": j}, device_id_type=MESH
            ).start()
            return carry

        lax.fori_loop(1, n, body, 0)

    def all_whole(buffer, index):
        rows = buffer.at[pl.ds(0, 2 * (n - 1))]
        return pltpu.make_async_remote_copy(
            rows, rows, asend.at[index], arecv.at[index], device_id={"seq": right}, device_id_type=MESH
        )

    def scatter_out(layer):
        all_send(
            lambda j: es.at[layer, lax.rem(j, 2), :, lax.div(j, 2)],
            r1[layer].at[pl.ds(2 * me, 2)],
            2 * layer,
        )
        r1[layer][pl.ds(2 * me, 2)] = es[layer, lax.rem(me, 2), :, lax.div(me, 2)]

    def forward_out(layer):
        all_whole(r1[layer], 2 * layer).wait_recv()

        def body(i, carry):
            s2[layer, 2 * i] = r1[layer][table[2 * i]]
            s2[layer, 2 * i + 1] = r1[layer][table[2 * i + 1]]
            return carry

        lax.fori_loop(0, n, body, 0)
        all_send(
            lambda j: s2.at[layer, pl.ds(2 * j, 2)],
            r2.at[layer, pl.ds(2 * me, 2)],
            2 * layer + 1,
        )
        r2[layer, pl.ds(2 * me, 2)] = s2[layer, pl.ds(2 * me, 2)]

    relays = n // 4
    relay = lax.rem(me, 4) == 3 * core
    relay_index = lax.div(me, 4)

    def key_part(count, index):
        rows = rr1.at[pl.ds(0, 2 * count)]
        return pltpu.make_async_remote_copy(
            rows, rows, asend.at[index], arecv.at[index], device_id={"seq": right}, device_id_type=MESH
        )

    def key_scatter():
        def body(m, carry):
            j = 4 * m + 3 * core
            r = 2 * m + core

            @pl.when(j != me)
            def _():
                pltpu.make_async_remote_copy(
                    er.at[:, r],
                    rr1.at[pl.ds(2 * me, 2)],
                    asend.at[4],
                    arecv.at[4],
                    device_id={"seq": j},
                    device_id_type=MESH,
                ).start()

            return carry

        lax.fori_loop(0, relays, body, 0)

        @pl.when(relay)
        def _():
            rr1[pl.ds(2 * me, 2)] = er[:, 2 * relay_index + core]

    def key_forward():
        @pl.when(relay)
        def _():
            key_part(n - 1, 4).wait_recv()

            def body(i, carry):
                rs2[2 * i] = rr1[table[2 * i]]
                rs2[2 * i + 1] = rr1[table[2 * i + 1]]
                return carry

            lax.fori_loop(0, n, body, 0)
            all_send(
                lambda j: rs2.at[pl.ds(2 * j, 2)],
                rr2.at[pl.ds(2 * relay_index, 2)],
                5,
            )
            rr2[pl.ds(2 * relay_index, 2)] = rs2[pl.ds(2 * me, 2)]

    def key_wait():
        @pl.when(relay)
        def _():
            key_part(relays - 1, 5).wait_recv()
            key_part(n - 1, 5).wait_send()
            key_part(relays - 1, 4).wait_send()

        @pl.when(jnp.logical_not(relay))
        def _():
            key_part(relays, 5).wait_recv()
            key_part(relays, 4).wait_send()

    def out_copy(layer):
        return pltpu.make_async_copy(ov.at[layer], out.at[layer], osem.at[layer])

    def arrange(layer):
        for h in range(2):
            for a in range(2):
                def tiles(ref):
                    rows = [ref[layer, 4 * r + 2 * h + a].astype(F32) for r in range(span // 8)]
                    return jnp.concatenate(rows, axis=0)

                mine, theirs = tiles(r2), tiles(rp)
                low = jnp.where(core == 0, mine, theirs).astype(BF16)
                high = jnp.where(core == 0, theirs, mine).astype(BF16)
                rows = slice(a * span, (a + 1) * span)
                ov[layer, rows, 2 * h * LANES : (2 * h + 1) * LANES] = low
                ov[layer, rows, (2 * h + 1) * LANES : (2 * h + 2) * LANES] = high

    def arrange_keys():
        for a in range(2):
            rows = []
            for r in range(span // 8):
                at = 2 * (r // 2) + a
                mine, theirs = rr2[at].astype(F32), rrp[at].astype(F32)
                rows.append(jnp.where(core == r % 2, mine, theirs))
            keys = jnp.concatenate(rows, axis=0).astype(BF16)
            where = slice(a * span, (a + 1) * span)
            ov[0, where, LAT:] = keys[:, :ROPE]
            ov[1, where, LAT:] = keys[:, ROPE:]

    work = [functools.partial(planes, q) for q in range(cols // 2)]
    step = 1
    for q in range(0, len(work), 2):
        for w in work[q : q + 2]:
            w()
        service(step)
        step += 1
    first_pair = pair_copy(cacc, cgot.at[pl.ds(0, 2)], 0)
    first_pair.start()
    trig_tables()
    service(step)
    step += 1
    first_pair.wait()
    first_gates()
    service(step)
    step += 1
    spread_gates()
    wanted_table()
    service(step)
    step += 1
    combine_rows(0, tokens // 32, 0)
    service(step)
    step += 1
    combine_rows(tokens // 32, tokens // 16, 0)
    service(step)
    step += 1
    cacc[...] = jnp.zeros_like(cacc)
    pp[...] = jnp.zeros_like(pp)
    for j in range(WAYS):
        pp[j * 8 : j * 8 + WAYS, :] = pre[j].astype(F32)
    while step <= half:
        service(step)
        step += 1
    cross_whole(5).wait_recv()
    cross_whole(6).wait_recv()

    down_project(0)
    pair_copy(down.at[0], got.at[0], 1).start()
    o_load().wait()
    pair_copy(down.at[0], got.at[0], 1).wait()
    entry(0)
    scatter_out(0)
    for tile in range(width // 512):
        update_tile(tile)
        if tile == 4:
            forward_out(0)
    second_pair = pair_copy(cacc, cgot.at[pl.ds(2, 2)], 2)
    second_pair.start()
    second_pair.wait()
    second_gates()
    combine_rows(0, tokens // 16, 0)
    cross_whole(7).wait_recv()
    cross_whole(8).wait_recv()
    down_project(1)
    pair_copy(down.at[1], got.at[1], 3).start()
    pair_copy(down.at[1], got.at[1], 3).wait()
    entry(1)
    key_scatter()
    scatter_out(1)
    all_whole(r2.at[0], 1).wait_recv()
    pair_copy(r2.at[0], rp.at[0], 4).start()
    pair_copy(r2.at[0], rp.at[0], 4).wait()
    arrange(0)
    key_forward()
    forward_out(1)
    for slot in FIRST + SECOND:
        for way in (0, 1):
            z_whole(way, slot).wait_send()
    for other in (5, 6, 7, 8):
        cross_whole(other).wait_send()
    for layer in range(2):
        all_whole(r1[layer], 2 * layer).wait_send()
    all_whole(r1[0], 1).wait_send()
    key_wait()
    pair_copy(rr2, rrp, 5).start()
    all_whole(r2.at[1], 3).wait_recv()
    pair_copy(r2.at[1], rp.at[1], 6).start()
    pair_copy(rr2, rrp, 5).wait()
    arrange_keys()
    out_copy(0).start()
    pair_copy(r2.at[1], rp.at[1], 6).wait()
    arrange(1)
    out_copy(1).start()
    all_whole(r1[1], 3).wait_send()
    out_copy(0).wait()
    out_copy(1).wait()


def solution(mesh):
    n = mesh.shape["seq"]
    groups = mesh.shape["groups"]
    ny = 2 ** math.ceil(math.log2(groups) / 2)

    def on_device(
        streams, mix_first, bias1, pre_second, bias2, w_latent, gain, out_weight, slots, owners, length
    ):
        tokens, ways, width = streams.shape
        chunk = w_latent.shape[1]
        cols = width // LANES
        full = n * chunk
        freq = THETA ** (-(np.arange(LANES) % (ROPE // 2)) / (ROPE // 2))
        vmem = pl.BlockSpec(memory_space=pltpu.VMEM)
        smem = pl.BlockSpec(memory_space=pltpu.SMEM)
        hbm = pl.BlockSpec(memory_space=pl.ANY)
        bias_row = jnp.pad(bias1[None, :], ((0, 0), (0, LANES - bias1.shape[0])))
        return pl.pallas_call(
            functools.partial(kernel, n, ny),
            out_shape=jax.ShapeDtypeStruct((2, tokens, LAT + ROPE), BF16),
            in_specs=[hbm, hbm, vmem, hbm, hbm, vmem, smem, vmem, vmem, smem, smem, smem],
            out_specs=hbm,
            scratch_shapes=[
                pltpu.VMEM((cols, tokens, ways, LANES), BF16),
                pltpu.VMEM((ways, tokens, width), BF16),
                pltpu.VMEM((9, full, LANES), BF16),
                pltpu.VMEM((2, chunk, LAT + ROPE), BF16),
                pltpu.VMEM((ways * 32, width), BF16),
                pltpu.VMEM((ways * 8, width), F32),
                pltpu.VMEM((tokens, width), BF16),
                pltpu.VMEM((LAT, width), BF16),
                pltpu.VMEM((2, tokens, LANES), F32),
                pltpu.VMEM((4, tokens, LANES), F32),
                pltpu.VMEM((LANES, tokens), F32),
                pltpu.VMEM((24, tokens, LANES), F32),
                pltpu.VMEM((2, tokens, LAT + LANES), F32),
                pltpu.VMEM((2, tokens, LAT + LANES), F32),
                pltpu.VMEM((tokens, LAT), BF16),
                pltpu.VMEM((tokens, 512), F32),
                pltpu.VMEM((2, tokens, LANES), F32),
                pltpu.VMEM((2, 2, 2, tokens // 16, 8, LANES), BF16),
                pltpu.VMEM((2, tokens // 16, 8, LANES), BF16),
                pltpu.VMEM((2 * n, 8, LANES), BF16),
                pltpu.VMEM((2 * n, 8, LANES), BF16),
                pltpu.VMEM((2, 2 * n, 8, LANES), BF16),
                pltpu.VMEM((2, 2 * n, 8, LANES), BF16),
                pltpu.VMEM((2, 2 * n, 8, LANES), BF16),
                pltpu.VMEM((2 * n, 8, LANES), BF16),
                pltpu.VMEM((2 * n, 8, LANES), BF16),
                pltpu.VMEM((n // 2, 8, LANES), BF16),
                pltpu.VMEM((n // 2, 8, LANES), BF16),
                pltpu.VMEM((2, tokens, LAT + ROPE), BF16),
                pltpu.SMEM((2 * n,), jnp.int32),
                pltpu.SemaphoreType.DMA((6 + cols,)),
                pltpu.SemaphoreType.DMA((2, 5)),
                pltpu.SemaphoreType.DMA((2, n // 2, 5)),
                pltpu.SemaphoreType.DMA((4,)),
                pltpu.SemaphoreType.DMA((4,)),
                pltpu.SemaphoreType.DMA((7,)),
                pltpu.SemaphoreType.DMA((7,)),
                pltpu.SemaphoreType.DMA((6,)),
                pltpu.SemaphoreType.DMA((6,)),
                pltpu.SemaphoreType.DMA((2,)),
            ],
            compiler_params=pltpu.CompilerParams(
                collective_id=0, has_side_effects=True, vmem_limit_bytes=61 * 2**20
            ),
        )(
            streams,
            jnp.transpose(mix_first, (0, 2, 1)),
            jnp.transpose(pre_second, (0, 2, 1)),
            w_latent,
            out_weight,
            bias_row,
            bias2,
            gain,
            jnp.asarray(freq[None, :], F32),
            slots,
            owners,
            length,
        )

    placed = (
        P(("groups", "seq"), None, "pd"),
        P(None, "pd", None),
        P(),
        P(None, "pd", None),
        P(),
        P(None, ("pd", "seq"), None),
        P(),
        P(None, "pd"),
        P("groups"),
        P("groups"),
        P("groups"),
    )
    return jax.shard_map(
        on_device, mesh=mesh, in_specs=placed, out_specs=P(None, ("groups", "seq"), None), check_vma=False
    )
```

time: 584 us -> 173 us (0.30)
  the two profiles are of different devices: /device:TPU:38 before, /device:TPU:45 now
where the time goes in v1:
time: 173 us
  Pallas kernels  169 us (98%)
  local copies, waits for them, and re-layouts  3.31 us (2%)
    pallas_call x1, Pallas kernels, on_device(): pl.pallas_call(functools.partial(kernel, n, ny), out_shape=jax.ShapeDtype...  169 us

profile of v1, /device:TPU:45, one launch (start us, length us, event | category | flops | bytes accessed | tf_op | source)
XLA Modules:
  0.0 172.6 jit_solution(1554283663169028095)
XLA Ops:
  0.7 1.2 pad.4.bias1
  1.8 168.7 %shard_map.118 = bf16[2,256,576]{2,1,0:T(8,128)(2,1)} custom-call(bf16[256,4,3584]{2,1,0:T(4,128)(2,1)} %streams.1, bf16[4,24,3584]{2,1,0:T(8,128)(2,1)} %bitcast.3, bf16[4,4,3584]{2,1,0:T(4,128)(2,1)} %bitcast.4, bf16[2,112,576]{2,1,0:T(8,128)(2,1)} %w_in.1, bf16[512,3584]{1,0:T(8,128)(2,1)} %out_w.1, f32[1,128]{1,0:T(1,128)} %pad.4.bias1, f32[4]{0:T(128)} %bias2.1, ...), custom_call_target="tpu_custom_call" | custom-call | tf_op jit(solution)/shard_map/pallas_call | solution.py:659
  170.5 2.1 %copy.13 = bf16[2,256,576]{1,2,0:T(8,128)(2,1)} copy(bf16[2,256,576]{2,1,0:T(8,128)(2,1)} %shard_map.118) | data formatting | bytes 1179648 | tf_op jit(solution)/shard_map/pallas_call | solution.py:659
